TPU v7x, 32 devices: a whole 2x2x4 slice. The times are simulated.
32 devices in a mesh: row: 4 (over z), col: 8 (over y, x, core).
Axes of the slice: x: 2, y: 2, z: 4, core: 2. Of those that a mesh axis runs over, the one named last changes fastest.
Arguments:
- node_latent: bfloat16 [32768, 128], P(('row', 'col')), may hold values from -6 to 6
- edge_latent: bfloat16 [131072, 128], P(('row', 'col')), may hold values from -6 to 6
- senders: int32 [131072], P(('row', 'col')), may hold values from 0 to 1535
- receivers: int32 [131072], P(('row', 'col')), may hold values from 0 to 1023
- send_index: int32 [32, 4, 128], P(('row', 'col')), may hold values from 0 to 1023
- context_table: bfloat16 [256, 128], P(('row', 'col')), may hold values from -6 to 6
- region: int32 [32768], P(('row', 'col')), may hold values from 0 to 255
- edge_w1: bfloat16 [2, 384, 128], replicated, may hold values from -0.3125 to 0.3125
- edge_w2: bfloat16 [2, 128, 128], replicated, may hold values from -0.5 to 0.5
- edge_bias: float32 [2, 3, 128], replicated, may hold values from -3 to 3
- edge_gain: float32 [2, 128], replicated, may hold values from 0.25 to 1.75
- node_w1: bfloat16 [2, 384, 128], replicated, may hold values from -0.3125 to 0.3125
- node_wg: bfloat16 [2, 128, 128], replicated, may hold values from -0.5 to 0.5
- node_w2: bfloat16 [2, 128, 128], replicated, may hold values from -0.5 to 0.5
- node_bias: float32 [2, 3, 128], replicated, may hold values from -3 to 3
- node_gain: float32 [2, 128], replicated, may hold values from 0.25 to 1.75
Outputs:
- node_out: bfloat16 [32768, 128], P(('row', 'col'))
- edge_out: bfloat16 [131072, 128], P(('row', 'col'))
Inputs may be any that keep to these rules, and one draw needn't show every extreme that they name: senders index the extended table of the edge's own partition: below 1024 its own nodes, then the four received blocks of 128 rows in the order above, below, left, right. receivers are nodes of the edge's own partition. `send_index`: rows of the sending partition's own nodes; repeats may occur.
All inputs are finite; a program needn't handle non-finite values.
Results may differ from a plain program's by a relative error of at most 0.0085.
Values may be sent and summed in bfloat16 or wider, within the bound.
A program may use at most 64 MiB of HBM per device.

v0:
```python
import math

import jax
import jax.numpy as jnp
from jax import lax
from jax.sharding import PartitionSpec as P

LAYERS = 2


EPS = 1e-05


def passed_along(value, axis, by):
    devices = lax.axis_size(axis)
    pairs = [(i, i + by) for i in range(devices) if 0 <= i + by < devices]
    return lax.ppermute(value, axis, pairs)


def norm_tail(pre, w_out, b_out, gain, shift):
    hidden = jax.nn.relu(pre).astype(jnp.bfloat16)
    y_val = jnp.dot(hidden, w_out, preferred_element_type=jnp.float32) + b_out
    centred = y_val - jnp.mean(y_val, axis=-1, keepdims=True)
    spread = jnp.mean(centred * centred, axis=-1, keepdims=True)
    return centred * lax.rsqrt(spread + EPS) * gain + shift


def one_hot(index, count):
    columns = lax.broadcasted_iota(jnp.int32, (1, count), 1)
    return (index[:, None] == columns).astype(jnp.bfloat16)


def lookup(index, table):
    picker = one_hot(index, table.shape[0])
    return jnp.dot(picker, table, preferred_element_type=jnp.float32).astype(jnp.bfloat16)


def blocked_lookup(index, table):
    total_rows = index.shape[0]
    block_rows = math.gcd(total_rows, 512)
    pieces = index.reshape(total_rows // block_rows, block_rows)
    result = lax.map(lambda piece: lookup(piece, table), pieces)
    return result.reshape(total_rows, table.shape[1])


def edge_and_sum(extended, nodes, edges, senders, receivers, w_in, w_out, bias, gain):
    total_rows = edges.shape[0]
    width = edges.shape[1]
    node_count = nodes.shape[0]
    block_rows = math.gcd(total_rows, 512)
    blocks = total_rows // block_rows

    def one_block(summed, items):
        edge_rows, send_rows, recv_rows = items
        recv_hot = one_hot(recv_rows, node_count)
        sender_feats = lookup(send_rows, extended)
        receiver_feats = jnp.dot(recv_hot, nodes, preferred_element_type=jnp.float32).astype(
            jnp.bfloat16
        )
        feats = jnp.concatenate([sender_feats, receiver_feats, edge_rows], axis=1)
        pre = jnp.dot(feats, w_in, preferred_element_type=jnp.float32) + bias[0]
        fresh = (
            edge_rows.astype(jnp.float32) + norm_tail(pre, w_out, bias[1], gain, bias[2])
        ).astype(jnp.bfloat16)
        added = lax.dot_general(
            recv_hot, fresh, (((0,), (0,)), ((), ())), preferred_element_type=jnp.float32
        )
        return (summed + added, fresh)

    start = jnp.zeros((node_count, width), jnp.float32)
    items = (
        edges.reshape(blocks, block_rows, width),
        senders.reshape(blocks, block_rows),
        receivers.reshape(blocks, block_rows),
    )
    summed, fresh = lax.scan(one_block, start, items)
    return (fresh.reshape(total_rows, width), summed.astype(jnp.bfloat16))


def node_step(nodes, summed, context_rows, w_in, w_out, bias, gain, shift_in):
    feats = jnp.concatenate([nodes, summed, context_rows], axis=1)
    pre = jnp.dot(feats, w_in, preferred_element_type=jnp.float32) + shift_in
    return (nodes.astype(jnp.float32) + norm_tail(pre, w_out, bias[1], gain, bias[2])).astype(
        jnp.bfloat16
    )


def row_move(block, offset):
    return passed_along(block, "row", offset)


def col_move(block, offset):
    return passed_along(block, "col", offset)


def extend(nodes, send_index):
    count = send_index.shape[2]
    width = nodes.shape[1]
    picked = lookup(send_index.reshape(-1), nodes).reshape(4, count, width)
    return jnp.concatenate(
        [
            nodes,
            row_move(picked[0], 1),
            row_move(picked[1], -1),
            col_move(picked[2], 1),
            col_move(picked[3], -1),
        ],
        axis=0,
    )


def local(
    node_latent,
    edge_latent,
    senders,
    receivers,
    send_index,
    context_table,
    region,
    edge_w1,
    edge_w2,
    edge_bias,
    edge_gain,
    node_w1,
    node_wg,
    node_w2,
    node_bias,
    node_gain,
):
    width = node_latent.shape[1]
    local_sum = jnp.sum(node_latent.astype(jnp.float32), axis=0)
    total = lax.psum(local_sum, ("row", "col"))
    by_row = lax.all_gather(context_table[None], "row", axis=0, tiled=True)
    table = lax.all_gather(by_row, "col", axis=1, tiled=True).reshape(-1, width)
    node_count = node_latent.shape[0] * lax.axis_size("row") * lax.axis_size("col")
    pooled = total / math.sqrt(node_count)
    context_rows = blocked_lookup(region, table)
    nodes = node_latent
    edges = edge_latent
    for layer in range(LAYERS):
        extended = extend(nodes, send_index)
        edges, summed = edge_and_sum(
            extended,
            nodes,
            edges,
            senders,
            receivers,
            edge_w1[layer],
            edge_w2[layer],
            edge_bias[layer],
            edge_gain[layer],
        )
        shift_in = node_bias[layer, 0] + jnp.dot(
            pooled, node_wg[layer].astype(jnp.float32), precision=lax.Precision.HIGHEST
        )
        nodes = node_step(
            nodes,
            summed,
            context_rows,
            node_w1[layer],
            node_w2[layer],
            node_bias[layer],
            node_gain[layer],
            shift_in,
        )
    return (nodes, edges)


def solution(mesh):
    return jax.shard_map(
        local,
        mesh=mesh,
        in_specs=(
            P(("row", "col"), None),
            P(("row", "col"), None),
            P(("row", "col")),
            P(("row", "col")),
            P(("row", "col"), None, None),
            P(("row", "col"), None),
            P(("row", "col")),
            P(),
            P(),
            P(),
            P(),
            P(),
            P(),
            P(),
            P(),
            P(),
        ),
        out_specs=(P(("row", "col"), None), P(("row", "col"), None)),
        check_vma=False,
    )
```

profile of v0, /device:TPU:11, one launch (start us, length us, event | category | flops | bytes accessed | tf_op | source)
XLA Modules:
  0.0 200.9 jit_solution(13532602859649688257)
XLA Ops:
  0.7 1.5 fusion.61
  2.9 3.2 %collective-permute-start = (bf16[128,128]{1,0:T(8,128)(2,1)}, bf16[128,128]{1,0:T(8,128)(2,1)S(1)}, u32[]{:S(2)}, u32[]{:S(2)}) collective-permute-start(bf16[128,128]{1,0:T(8,128)(2,1)} %get-tuple-element.356), channel_id=1, source_target_pairs={{0,8},{8,16},{16,24},{1,9},{9,17},{17,25},{2,10},{10,18},{18,26},{... | collective-permute-start | bytes 98312 | tf_op jit(solution)/shard_map/ppermute | solution.py:17
  6.1 2.1 %collective-permute-start.1 = (bf16[128,128]{1,0:T(8,128)(2,1)}, bf16[128,128]{1,0:T(8,128)(2,1)S(1)}, u32[]{:S(2)}, u32[]{:S(2)}) collective-permute-start(bf16[128,128]{1,0:T(8,128)(2,1)} %get-tuple-element.355), channel_id=1, source_target_pairs={{8,0},{16,8},{24,16},{9,1},{17,9},{25,17},{10,2},{18,10},{26,18},{... | collective-permute-start | bytes 98312 | tf_op jit(solution)/shard_map/ppermute | solution.py:17
  8.2 4.2 %collective-permute-start.2 = (bf16[128,128]{1,0:T(8,128)(2,1)S(1)}, bf16[128,128]{1,0:T(8,128)(2,1)S(1)}, u32[]{:S(2)}, u32[]{:S(2)}) collective-permute-start(bf16[128,128]{1,0:T(8,128)(2,1)S(1)} %get-tuple-element.354), channel_id=1, source_target_pairs={{0,1},{1,2},{2,3},{3,4},{4,5},{5,6},{6,7},{8,9},{9,10},{10,11},{11... | collective-permute-start | bytes 98312 | tf_op jit(solution)/shard_map/ppermute | solution.py:17
  12.4 1.9 collective-permute-start.3
  15.4 40.4 %psum.7 = f32[128]{0:T(128)S(1)} all-reduce(f32[128]{0:T(128)S(1)} %convert_reduce_fusion), channel_id=1, replica_groups=mesh['row'=4,'col'=8] {'row','col'}, use_global_device_ids=true, to_apply=%region_7.8 | all-reduce | flops 128 | bytes 1024 | tf_op jit(solution)/shard_map/psum | solution.py:132
  56.3 8.2 %all-gather = bf16[32,128]{1,0:T(8,128)(2,1)S(1)} all-gather(bf16[8,128]{1,0:T(8,128)(2,1)S(1)} %copy-done.10), channel_id=2, replica_groups=mesh['row'=4,'col'=8] {'row'}, dimensions={0}, use_global_device_ids=true | all-gather | bytes 10240 | tf_op jit(solution)/shard_map/all_gather | solution.py:133
  64.5 12.8 %all_gather.7 = bf16[4,64,128]{2,1,0:T(8,128)(2,1)S(1)} all-gather(bf16[4,8,128]{2,1,0:T(8,128)(2,1)S(1)} %bitcast.189), channel_id=1, replica_groups=mesh['row'=4,'col'=8] {'col'}, dimensions={1}, use_global_device_ids=true | all-gather | bytes 73728 | tf_op jit(solution)/shard_map/all_gather | solution.py:134
  79.1 50.7 %while.37 = (s32[]{:T(128)}, f32[1024,128]{1,0:T(8,128)S(1)}, bf16[8,512,128]{1,2,0:T(8,128)(2,1)S(1)}, s32[8,512]{1,0:T(8,128)S(1)}, bf16[8,512,128]{2,1,0:T(8,...) while((s32[]{:T(128)}, f32[1024,128]{1,0:T(8,128)S(1)}, ...), condition=%wide.region_3.4_spmd.clone, body=%wide.region_0.3_spmd.clone.sunk | while | flops 541786624 | bytes 4363419 | solution.py:76
  80.4 1.5 fusion.176
  86.7 1.5 fusion.176
  93.1 1.5 fusion.176
  99.4 1.5 fusion.176
  105.7 1.5 fusion.176
  112.0 1.5 fusion.176
  118.4 1.5 fusion.176
  124.7 1.5 fusion.176
  129.9 1.5 fusion.125
  132.8 2.8 %collective-permute-start.4 = (bf16[128,128]{0,1:T(8,128)(2,1)S(1)}, bf16[128,128]{0,1:T(8,128)(2,1)S(1)}, u32[]{:S(2)}, u32[]{:S(2)}) collective-permute-start(bf16[128,128]{0,1:T(8,128)(2,1)S(1)} %get-tuple-element.352), channel_id=1, source_target_pairs={{0,8},{8,16},{16,24},{1,9},{9,17},{17,25},{2,10},{10,18},{18,26},{... | collective-permute-start | bytes 98312 | tf_op jit(solution)/shard_map/ppermute | solution.py:17
  136.5 2.5 %collective-permute-start.5 = (bf16[128,128]{0,1:T(8,128)(2,1)S(1)}, bf16[128,128]{0,1:T(8,128)(2,1)S(1)}, u32[]{:S(2)}, u32[]{:S(2)}) collective-permute-start(bf16[128,128]{0,1:T(8,128)(2,1)S(1)} %get-tuple-element.351), channel_id=1, source_target_pairs={{8,0},{16,8},{24,16},{9,1},{17,9},{25,17},{10,2},{18,10},{26,18},{... | collective-permute-start | bytes 98312 | tf_op jit(solution)/shard_map/ppermute | solution.py:17
  139.1 3.7 %collective-permute-start.6 = (bf16[128,128]{0,1:T(8,128)(2,1)S(1)}, bf16[128,128]{0,1:T(8,128)(2,1)S(1)}, u32[]{:S(2)}, u32[]{:S(2)}) collective-permute-start(bf16[128,128]{0,1:T(8,128)(2,1)S(1)} %get-tuple-element.350), channel_id=1, source_target_pairs={{0,1},{1,2},{2,3},{3,4},{4,5},{5,6},{6,7},{8,9},{9,10},{10,11},{11... | collective-permute-start | bytes 98312 | tf_op jit(solution)/shard_map/ppermute | solution.py:17
  142.8 1.9 collective-permute-start.7
  144.8 4.1 %collective-permute-done.7 = bf16[128,128]{0,1:T(8,128)(2,1)S(1)} collective-permute-done((bf16[128,128]{0,1:T(8,128)(2,1)S(1)}, bf16[128,128]{0,1:T(8,128)(2,1)S(1)}, u32[]{:S(2)}, u32[]{:S(2)}) %collective-permute-start.7) | collective-permute-done | bytes 32800 | tf_op jit(solution)/shard_map/ppermute | solution.py:17
  149.2 49.0 %while.38 = (s32[]{:T(128)}, f32[1024,128]{1,0:T(8,128)S(1)}, bf16[8,512,128]{2,1,0:T(8,128)(2,1)}, s32[8,512]{1,0:T(8,128)S(1)}, bf16[8,512,128]{1,2,0:T(8,128)...) while((s32[]{:T(128)}, f32[1024,128]{1,0:T(8,128)S(1)}, ...), condition=%wide.region_13.14_spmd.clone, body=%wide.region_10.13_spmd.clone.sunk | while | flops 541786624 | bytes 4495003 | solution.py:76
  150.5 1.5 fusion.186
  156.6 1.5 fusion.186
  162.7 1.5 fusion.186
  168.8 1.5 fusion.186
  175.0 1.5 fusion.186
  181.1 1.5 fusion.186
  187.2 1.5 fusion.186
  193.3 1.5 fusion.186
  (281 shorter events, 84.0 us)
Async XLA Ops:
  0.6 13.7 %copy-start = (bf16[1024,128]{1,0:T(8,128)(2,1)S(1)}, bf16[1024,128]{1,0:T(8,128)(2,1)}, u32[]{:S(2)}) copy-start(bf16[1024,128]{1,0:T(8,128)(2,1)} %param.22) | copy-start | bytes 786436
  0.6 13.9 %copy-start.1 = (bf16[2,384,128]{2,1,0:T(8,128)(2,1)S(1)}, bf16[2,384,128]{2,1,0:T(8,128)(2,1)}, u32[]{:S(2)}) copy-start(bf16[2,384,128]{2,1,0:T(8,128)(2,1)} %param.29) | copy-start | bytes 589828
  0.7 13.9 %copy-start.2 = (bf16[2,128,128]{2,1,0:T(8,128)(2,1)S(1)}, bf16[2,128,128]{2,1,0:T(8,128)(2,1)}, u32[]{:S(2)}) copy-start(bf16[2,128,128]{2,1,0:T(8,128)(2,1)} %param.30) | copy-start | bytes 196612
  0.7 14.5 %copy-start.7 = (f32[2,3,128]{2,0,1:T(2,128)S(1)}, f32[2,3,128]{2,0,1:T(2,128)}, u32[]{:S(2)}) copy-start(f32[2,3,128]{2,0,1:T(2,128)} %param.31) | copy-start | bytes 9220
  0.7 14.5 %copy-start.12 = (f32[2,128]{1,0:T(2,128)S(1)}, f32[2,128]{1,0:T(2,128)}, u32[]{:S(2)}) copy-start(f32[2,128]{1,0:T(2,128)} %param.32) | copy-start | bytes 3076
  2.2 53.5 %copy-start.11 = (f32[2,3,128]{2,0,1:T(2,128)S(1)}, f32[2,3,128]{2,0,1:T(2,128)}, u32[]{:S(2)}) copy-start(f32[2,3,128]{2,0,1:T(2,128)} %param.36) | copy-start | bytes 9220
  2.2 54.1 %copy-start.10 = (bf16[8,128]{1,0:T(8,128)(2,1)S(1)}, bf16[8,128]{1,0:T(8,128)(2,1)}, u32[]{:S(2)}) copy-start(bf16[8,128]{1,0:T(8,128)(2,1)} %param.27) | copy-start | bytes 6148
  2.2 75.0 %copy-start.6 = (s32[1024]{0:T(1024)S(1)}, s32[1024]{0:T(1024)}, u32[]{:S(2)}) copy-start(s32[1024]{0:T(1024)} %param.28) | copy-start | bytes 12292
  2.9 76.1 %collective-permute-start = (bf16[128,128]{1,0:T(8,128)(2,1)}, bf16[128,128]{1,0:T(8,128)(2,1)S(1)}, u32[]{:S(2)}, u32[]{:S(2)}) collective-permute-start(bf16[128,128]{1,0:T(8,128)(2,1)} %get-tuple-element.356), channel_id=1, source_target_pairs={{0,8},{8,16},{16,24},{1,9},{9,17},{17,25},{2,10},{10,18},{18,26},{... | collective-permute-start | bytes 98312 | tf_op jit(solution)/shard_map/ppermute | solution.py:17
  6.1 72.9 %collective-permute-start.1 = (bf16[128,128]{1,0:T(8,128)(2,1)}, bf16[128,128]{1,0:T(8,128)(2,1)S(1)}, u32[]{:S(2)}, u32[]{:S(2)}) collective-permute-start(bf16[128,128]{1,0:T(8,128)(2,1)} %get-tuple-element.355), channel_id=1, source_target_pairs={{8,0},{16,8},{24,16},{9,1},{17,9},{25,17},{10,2},{18,10},{26,18},{... | collective-permute-start | bytes 98312 | tf_op jit(solution)/shard_map/ppermute | solution.py:17
  8.2 70.8 %collective-permute-start.2 = (bf16[128,128]{1,0:T(8,128)(2,1)S(1)}, bf16[128,128]{1,0:T(8,128)(2,1)S(1)}, u32[]{:S(2)}, u32[]{:S(2)}) collective-permute-start(bf16[128,128]{1,0:T(8,128)(2,1)S(1)} %get-tuple-element.354), channel_id=1, source_target_pairs={{0,1},{1,2},{2,3},{3,4},{4,5},{5,6},{6,7},{8,9},{9,10},{10,11},{11... | collective-permute-start | bytes 98312 | tf_op jit(solution)/shard_map/ppermute | solution.py:17
  12.4 66.6 %collective-permute-start.3 = (bf16[128,128]{1,0:T(8,128)(2,1)S(1)}, bf16[128,128]{1,0:T(8,128)(2,1)S(1)}, u32[]{:S(2)}, u32[]{:S(2)}) collective-permute-start(bf16[128,128]{1,0:T(8,128)(2,1)S(1)} %get-tuple-element.353), channel_id=1, source_target_pairs={{1,0},{2,1},{3,2},{4,3},{5,4},{6,5},{7,6},{9,8},{10,9},{11,10},{12... | collective-permute-start | bytes 98312 | tf_op jit(solution)/shard_map/ppermute | solution.py:17
  15.2 62.7 %copy-start.13 = (f32[2,128]{1,0:T(2,128)S(1)}, f32[2,128]{1,0:T(2,128)}, u32[]{:S(2)}) copy-start(f32[2,128]{1,0:T(2,128)} %param.37) | copy-start | bytes 3076
  15.2 63.3 %copy-start.16 = (bf16[2,128,128]{2,1,0:T(8,128)(2,1)S(1)}, bf16[2,128,128]{2,1,0:T(8,128)(2,1)}, u32[]{:S(2)}) copy-start(bf16[2,128,128]{2,1,0:T(8,128)(2,1)} %param.34) | copy-start | bytes 196612
  77.3 1.5 copy-start.4
  77.3 1.5 copy-start.5
  129.9 1.7 copy-start.8
  129.9 1.7 copy-start.9
  131.4 0.7 copy-start.18
  131.5 4.0 %copy-start.17 = (bf16[2,128,128]{2,1,0:T(8,128)(2,1)S(1)}, bf16[2,128,128]{2,1,0:T(8,128)(2,1)}, u32[]{:S(2)}) copy-start(bf16[2,128,128]{2,1,0:T(8,128)(2,1)} %param.34) | copy-start | bytes 196612
  132.7 16.4 %copy-start.3 = (bf16[128,128]{1,0:T(8,128)(2,1)S(1)}, bf16[128,128]{1,0:T(8,128)(2,1)}, u32[]{:S(2)}) copy-start(bf16[128,128]{1,0:T(8,128)(2,1)} %get-tuple-element.643) | copy-start | bytes 98308
  132.8 11.9 %collective-permute-start.4 = (bf16[128,128]{0,1:T(8,128)(2,1)S(1)}, bf16[128,128]{0,1:T(8,128)(2,1)S(1)}, u32[]{:S(2)}, u32[]{:S(2)}) collective-permute-start(bf16[128,128]{0,1:T(8,128)(2,1)S(1)} %get-tuple-element.352), channel_id=1, source_target_pairs={{0,8},{8,16},{16,24},{1,9},{9,17},{17,25},{2,10},{10,18},{18,26},{... | collective-permute-start | bytes 98312 | tf_op jit(solution)/shard_map/ppermute | solution.py:17
  136.5 8.2 %collective-permute-start.5 = (bf16[128,128]{0,1:T(8,128)(2,1)S(1)}, bf16[128,128]{0,1:T(8,128)(2,1)S(1)}, u32[]{:S(2)}, u32[]{:S(2)}) collective-permute-start(bf16[128,128]{0,1:T(8,128)(2,1)S(1)} %get-tuple-element.351), channel_id=1, source_target_pairs={{8,0},{16,8},{24,16},{9,1},{17,9},{25,17},{10,2},{18,10},{26,18},{... | collective-permute-start | bytes 98312 | tf_op jit(solution)/shard_map/ppermute | solution.py:17
  139.1 5.7 %collective-permute-start.6 = (bf16[128,128]{0,1:T(8,128)(2,1)S(1)}, bf16[128,128]{0,1:T(8,128)(2,1)S(1)}, u32[]{:S(2)}, u32[]{:S(2)}) collective-permute-start(bf16[128,128]{0,1:T(8,128)(2,1)S(1)} %get-tuple-element.350), channel_id=1, source_target_pairs={{0,1},{1,2},{2,3},{3,4},{4,5},{5,6},{6,7},{8,9},{9,10},{10,11},{11... | collective-permute-start | bytes 98312 | tf_op jit(solution)/shard_map/ppermute | solution.py:17
  142.8 6.1 %collective-permute-start.7 = (bf16[128,128]{0,1:T(8,128)(2,1)S(1)}, bf16[128,128]{0,1:T(8,128)(2,1)S(1)}, u32[]{:S(2)}, u32[]{:S(2)}) collective-permute-start(bf16[128,128]{0,1:T(8,128)(2,1)S(1)} %get-tuple-element.349), channel_id=1, source_target_pairs={{1,0},{2,1},{3,2},{4,3},{5,4},{6,5},{7,6},{9,8},{10,9},{11,10},{12... | collective-permute-start | bytes 98312 | tf_op jit(solution)/shard_map/ppermute | solution.py:17
  149.1 49.1 %copy-start.14 = (f32[128]{0:T(128)S(1)}, f32[128]{0:T(128)}, u32[]{:S(2)}) copy-start(f32[128]{0:T(128)} %get-tuple-element.362) | copy-start | bytes 1540
  149.2 49.1 %copy-start.15 = (bf16[2,384,128]{2,1,0:T(8,128)(2,1)S(1)}, bf16[2,384,128]{2,1,0:T(8,128)(2,1)}, u32[]{:S(2)}) copy-start(bf16[2,384,128]{2,1,0:T(8,128)(2,1)} %param.33) | copy-start | bytes 589828
where the time goes:
time: 202 us; the launch traced here: 201 us
  matrix products  87.2 us (43%)
  blocking collectives  61.3 us (30%)
  starting transfers between devices  22.3 us (11%)
  local copies, waits for them, and re-layouts  19.7 us (10%)
  waiting for transfers between devices  4.14 us (2%)
  other arithmetic  3.71 us (2%)
    psum x1, blocking collectives, local(): total = lax.psum(local_sum, ('row', 'col'))  40.4 us
    dot_general x20, matrix products, lookup(): jnp.dot(picker, table, preferred_element_type=jnp.float32)  27 us
    dot_general x18, matrix products, norm_tail(): y_val = jnp.dot(hidden, w_out, preferred_element_type=jnp.float32) + b_out  26.1 us
    ppermute x8, starting transfers between devices, passed_along(): return lax.ppermute(value, axis, pairs)  22.3 us
    dot_general x16, matrix products, one_block(): jnp.dot(recv_hot, nodes, preferred_element_type=jnp.float32)  20.8 us
    all_gather x1, blocking collectives, local(): table = lax.all_gather(by_row, 'col', axis=1, tiled=True).reshape(-1, width)  12.8 us
    dot_general x16, matrix products, one_block(): lax.dot_general(recv_hot, fresh, (((0,), (0,)), ((), ())), preferred_elem...  12.3 us
    dynamic_slice x32, local copies, waits for them, and re-layouts, edge_and_sum(): summed, fresh = lax.scan(one_block, start, items)  8.37 us
  transfers between devices with their start and end apart: 8, of which 1 were waited for; matrix products, arithmetic and copies ran while one was open for 2% of the time, Pallas kernels for 0%

commit v1 on v0

v1 whole, which is shorter than its diff:
```python
import functools
import math

import jax
import jax.numpy as jnp
from jax import lax
from jax.experimental import pallas as pl
from jax.experimental.pallas import tpu as pltpu
from jax.sharding import PartitionSpec as P

LAYERS = 2
EPS = 1e-05
LANES = 128
BLOCK = 512
F32 = jnp.float32
BF16 = jnp.bfloat16
MESH = pl.DeviceIdType.MESH


def mm(a, b):
    return jnp.dot(a, b, preferred_element_type=F32)


def iota(axis):
    return lax.broadcasted_iota(jnp.int32, (LANES, LANES), axis)


def as_column(row):
    return jnp.transpose(jnp.broadcast_to(row, (LANES, LANES)))


def hot(mask):
    return jnp.where(mask, 1.0, 0.0).astype(BF16)


def pick_rows(column, count):
    lanes = iota(1)
    parts = [hot(column == lanes + start) for start in range(0, count, LANES)]
    return jnp.concatenate(parts, axis=1)


def norm(y_val, gain, shift):
    centred = y_val - jnp.mean(y_val, axis=-1, keepdims=True)
    spread = jnp.mean(centred * centred, axis=-1, keepdims=True)
    return centred * lax.rsqrt(spread + EPS) * gain + shift


def kernel(
    n_row,
    n_col,
    node_ref,
    edge_ref,
    send_ref,
    recv_ref,
    index_ref,
    ctx_ref,
    region_ref,
    ew1,
    ew2,
    eb,
    eg,
    nw1,
    nwg,
    nw2,
    nb,
    ng,
    node_out,
    edge_out,
    hot_send,
    hot_recv,
    hot_sum,
    side_send,
    side_recv,
    hot_index,
    picked,
    halo,
    table,
    from_ext,
    from_own,
    sums,
    ctx_part,
    halo_send_sem,
    halo_recv_sem,
    row_send_sem,
    row_recv_sem,
    col_send_sem,
    col_recv_sem,
):
    my_row, my_col = lax.axis_index("row"), lax.axis_index("col")
    nodes, width = node_ref.shape
    edges = edge_ref.shape[0]
    count = index_ref.shape[1]
    ext = nodes + 4 * count
    half_ext, half_own = ext // 2, nodes // 2
    ctx_rows = ctx_ref.shape[0]
    per_block = BLOCK // LANES

    barrier = pltpu.get_barrier_semaphore()
    for step in range(1, n_row):
        pl.semaphore_signal(
            barrier, inc=1, device_id=(lax.rem(my_row + step, n_row), my_col), device_id_type=MESH
        )
    for step in range(1, n_col):
        pl.semaphore_signal(
            barrier, inc=1, device_id=(my_row, lax.rem(my_col + step, n_col)), device_id_type=MESH
        )

    for side in range(4):
        rows = slice(side * count, (side + 1) * count)
        hot_index[rows, :] = pick_rows(as_column(index_ref[side : side + 1, :]), nodes)
    picked[0] = mm(hot_index[...], node_ref[...]).astype(BF16)
    part = jnp.sum(node_ref[...].astype(F32).reshape(nodes // 8, 8, width), axis=0)
    table[my_col, my_row] = jnp.concatenate([ctx_ref[...].astype(F32), part], axis=0)

    pl.semaphore_wait(barrier, n_row + n_col - 2)

    moves = (
        (my_row + 1, my_col, my_row < n_row - 1, my_row > 0),
        (my_row - 1, my_col, my_row > 0, my_row < n_row - 1),
        (my_row, my_col + 1, my_col < n_col - 1, my_col > 0),
        (my_row, my_col - 1, my_col > 0, my_col < n_col - 1),
    )

    def halo_copy(layer, side):
        to_row, to_col = moves[side][:2]
        rows = pl.ds(side * count, count)
        return pltpu.make_async_remote_copy(
            src_ref=picked.at[layer, rows],
            dst_ref=halo.at[layer, rows],
            send_sem=halo_send_sem.at[layer, side],
            recv_sem=halo_recv_sem.at[layer, side],
            device_id=(to_row, to_col),
            device_id_type=MESH,
        )

    def halo_start(layer):
        for side in range(4):

            @pl.when(moves[side][2])
            def _(side=side):
                halo_copy(layer, side).start()

    def halo_wait(layer):
        for side in range(4):

            @pl.when(moves[side][3])
            def _(side=side):
                halo_copy(layer, side).wait_recv()

            @pl.when(jnp.logical_not(moves[side][3]))
            def _(side=side):
                halo[layer, side * count : (side + 1) * count] = jnp.zeros((count, width), BF16)

    def row_copy(step, owner):
        return pltpu.make_async_remote_copy(
            src_ref=table.at[my_col, owner],
            dst_ref=table.at[my_col, owner],
            send_sem=row_send_sem.at[step - 1],
            recv_sem=row_recv_sem.at[step - 1],
            device_id=(lax.rem(my_row + step, n_row), my_col),
            device_id_type=MESH,
        )

    def col_copy(step, owner):
        return pltpu.make_async_remote_copy(
            src_ref=table.at[owner],
            dst_ref=table.at[owner],
            send_sem=col_send_sem.at[step - 1],
            recv_sem=col_recv_sem.at[step - 1],
            device_id=(my_row, lax.rem(my_col + step, n_col)),
            device_id_type=MESH,
        )

    halo_start(0)
    for step in range(1, n_row):
        row_copy(step, my_row).start()

    def prepare(block, carry):
        for sub in range(per_block):
            line = block * per_block + sub
            send_row = send_ref[pl.ds(line, 1), :]
            recv_row = recv_ref[pl.ds(line, 1), :]
            rows = pl.ds(pl.multiple_of(line * LANES, LANES), LANES)
            send = as_column(send_row)
            recv = as_column(recv_row)
            send_high = (send >= half_ext).astype(jnp.int32)
            recv_high = (recv >= half_own).astype(jnp.int32)
            side_send[rows, :] = send_high
            side_recv[rows, :] = recv_high
            hot_send[rows, :] = pick_rows(send - send_high * half_ext, half_ext)
            hot_recv[rows, :] = pick_rows(recv - recv_high * half_own, half_own)
            recv_low = recv_row - (recv_row >= half_own).astype(jnp.int32) * half_own
            for start in range(0, half_own, LANES):
                hot_sum[block, start : start + LANES, sub * LANES : (sub + 1) * LANES] = hot(
                    iota(0) + start == recv_low
                )
        return carry

    lax.fori_loop(0, edges // BLOCK, prepare, 0)

    for step in range(1, n_row):
        row_copy(step, lax.rem(my_row + n_row - step, n_row)).wait_recv()
    for step in range(1, n_col):
        col_copy(step, my_col).start()

    def fill_own(layer, now):
        w_pair = jnp.concatenate([ew1[layer, :width], ew1[layer, width : 2 * width]], axis=1)
        both = mm(now[...], w_pair).astype(BF16)
        from_ext[:, :width] = both[:half_ext, :width]
        from_ext[: nodes - half_ext, width:] = both[half_ext:, :width]
        from_own[:, :width] = both[:half_own, width:]
        from_own[:, width:] = both[half_own:, width:]

    def edge_phase(layer, source):
        from_ext[nodes - half_ext :, width:] = mm(halo[layer], ew1[layer, :width]).astype(BF16)
        sums[...] = jnp.zeros_like(sums)

        def body(block, carry):
            rows = pl.ds(pl.multiple_of(block * BLOCK, BLOCK), BLOCK)
            old = source[rows, :]
            by_send = mm(hot_send[rows, :], from_ext[...])
            by_recv = mm(hot_recv[rows, :], from_own[...])
            high = side_recv[rows, :] > 0
            pre = mm(old, ew1[layer, 2 * width :]) + eb[layer, 0:1]
            pre += jnp.where(side_send[rows, :] > 0, by_send[:, width:], by_send[:, :width])
            pre += jnp.where(high, by_recv[:, width:], by_recv[:, :width])
            hidden = jnp.maximum(pre, 0.0).astype(BF16)
            y_val = mm(hidden, ew2[layer]) + eb[layer, 1:2]
            new = old.astype(F32) + norm(y_val, eg[layer : layer + 1], eb[layer, 2:3])
            edge_out[rows, :] = new.astype(BF16)
            low_part = jnp.where(high, 0.0, new).astype(BF16)
            high_part = jnp.where(high, new, 0.0).astype(BF16)
            sums[...] += mm(hot_sum[block], jnp.concatenate([low_part, high_part], axis=1))
            return carry

        lax.fori_loop(0, edges // BLOCK, body, 0)

    def node_phase(layer, now, shift_in):
        summed = jnp.concatenate([sums[:, :width], sums[:, width:]], axis=0).astype(BF16)
        feats = jnp.concatenate([now[...], summed], axis=1)
        pre = mm(feats, nw1[layer, : 2 * width]) + shift_in
        pre += ctx_part[:, layer * width : (layer + 1) * width]
        hidden = jnp.maximum(pre, 0.0).astype(BF16)
        y_val = mm(hidden, nw2[layer]) + nb[layer, 1:2]
        new = now[...].astype(F32) + norm(y_val, ng[layer : layer + 1], nb[layer, 2:3])
        node_out[...] = new.astype(BF16)

    fill_own(0, node_ref)
    halo_wait(0)
    edge_phase(0, edge_ref)

    for step in range(1, n_col):
        col_copy(step, lax.rem(my_col + n_col - step, n_col)).wait_recv()
    pooled_sum = jnp.zeros((8, width), F32)
    shared = []
    for row in range(n_row):
        for col in range(n_col):
            shared.append(table[col, row, :ctx_rows])
            pooled_sum += table[col, row, ctx_rows:]
    pooled = jnp.sum(pooled_sum, axis=0, keepdims=True) / math.sqrt(nodes * n_row * n_col)
    regions = n_row * n_col * ctx_rows
    w_pair = jnp.concatenate([nw1[l, 2 * width :] for l in range(LAYERS)], axis=1)
    projected = mm(jnp.concatenate(shared, axis=0).astype(BF16), w_pair).astype(BF16)
    for line in range(nodes // LANES):
        picker = pick_rows(as_column(region_ref[line : line + 1, :]), regions)
        ctx_part[line * LANES : (line + 1) * LANES, :] = mm(picker, projected)
    shifts = [
        nb[l, 0:1]
        + jnp.dot(
            pooled, nwg[l].astype(F32), precision=lax.Precision.HIGHEST, preferred_element_type=F32
        )
        for l in range(LAYERS)
    ]
    node_phase(0, node_ref, shifts[0])

    picked[1] = mm(hot_index[...], node_out[...]).astype(BF16)
    halo_start(1)
    fill_own(1, node_out)
    halo_wait(1)
    edge_phase(1, edge_out)
    node_phase(1, node_out, shifts[1])

    for layer in range(LAYERS):
        for side in range(4):

            @pl.when(moves[side][2])
            def _(layer=layer, side=side):
                halo_copy(layer, side).wait_send()

    for step in range(1, n_row):
        row_copy(step, my_row).wait_send()
    for step in range(1, n_col):
        col_copy(step, my_col).wait_send()


def local(n_row, n_col, *args):
    node, edge, send, recv, index, ctx, region = args[:7]
    nodes, width = node.shape
    edges = edge.shape[0]
    count = index.shape[2]
    half_ext, half_own = (nodes + 4 * count) // 2, nodes // 2
    vmem = pl.BlockSpec(memory_space=pltpu.VMEM)
    dma = pltpu.SemaphoreType.DMA
    operands = (
        node,
        edge,
        send.reshape(edges // LANES, LANES),
        recv.reshape(edges // LANES, LANES),
        index.reshape(4, count),
        ctx,
        region.reshape(nodes // LANES, LANES),
    ) + args[7:]
    return pl.pallas_call(
        functools.partial(kernel, n_row, n_col),
        out_shape=(
            jax.ShapeDtypeStruct(node.shape, BF16),
            jax.ShapeDtypeStruct(edge.shape, BF16),
        ),
        in_specs=[vmem] * len(operands),
        out_specs=(vmem, vmem),
        scratch_shapes=[
            pltpu.VMEM((edges, half_ext), BF16),
            pltpu.VMEM((edges, half_own), BF16),
            pltpu.VMEM((edges // BLOCK, half_own, BLOCK), BF16),
            pltpu.VMEM((edges, width), jnp.int32),
            pltpu.VMEM((edges, width), jnp.int32),
            pltpu.VMEM((4 * count, nodes), BF16),
            pltpu.VMEM((LAYERS, 4 * count, width), BF16),
            pltpu.VMEM((LAYERS, 4 * count, width), BF16),
            pltpu.VMEM((n_col, n_row, ctx.shape[0] + 8, width), F32),
            pltpu.VMEM((half_ext, 2 * width), BF16),
            pltpu.VMEM((half_own, 2 * width), BF16),
            pltpu.VMEM((half_own, 2 * width), F32),
            pltpu.VMEM((nodes, LAYERS * width), F32),
            dma((LAYERS, 4)),
            dma((LAYERS, 4)),
            dma((n_row - 1,)),
            dma((n_row - 1,)),
            dma((n_col - 1,)),
            dma((n_col - 1,)),
        ],
        compiler_params=pltpu.CompilerParams(
            collective_id=0, has_side_effects=True, vmem_limit_bytes=56 * 1024 * 1024
        ),
        name="mesh_steps",
    )(*operands)


def solution(mesh):
    both = ("row", "col")
    split = (P(both, None), P(both, None), P(both), P(both), P(both, None, None), P(both, None), P(both))
    return jax.shard_map(
        functools.partial(local, mesh.shape["row"], mesh.shape["col"]),
        mesh=mesh,
        in_specs=split + (P(),) * 9,
        out_specs=(P(both, None), P(both, None)),
        check_vma=False,
    )
```

time: 202 us -> 45.8 us (0.23)
  the two profiles are of different devices: /device:TPU:11 before, /device:TPU:0 now
where the time goes in v1:
time: 45.8 us; the launch traced here: 45.5 us
  Pallas kernels  39 us (85%)
  local copies, waits for them, and re-layouts  5.89 us (13%)
  between operations  0.65 us (1%)
    pallas_call x1, Pallas kernels, local(): pl.pallas_call(functools.partial(kernel, n_row, n_col), out_shape=(jax.Sh...  39 us
    unnamed x8, local copies, waits for them, and re-layouts  5.89 us

profile of v1, /device:TPU:0, one launch (start us, length us, event | category | flops | bytes accessed | tf_op | source)
XLA Modules:
  0.0 45.5 jit_solution(2074966967011468500)
XLA Ops:
  0.6 0.0 copy-start
  0.6 0.7 %copy-done = f32[2,3,128]{2,0,1:T(2,128)S(1)} copy-done((f32[2,3,128]{2,0,1:T(2,128)S(1)}, f32[2,3,128]{2,0,1:T(2,128)}, u32[]{:S(2)}) %copy-start) | copy-done | bytes 3096
  1.3 0.0 copy-start.1
  1.3 0.6 %copy.18.eb = f32[2,3,128]{2,1,0:T(4,128)} copy(f32[2,3,128]{2,0,1:T(2,128)S(1)} %copy-done) | data formatting | bytes 6144 | tf_op args[9]
  1.9 0.1 copy-done.1
  2.0 0.6 %copy.19.nb = f32[2,3,128]{2,1,0:T(4,128)} copy(f32[2,3,128]{2,0,1:T(2,128)S(1)} %copy-done.1) | data formatting | bytes 6144 | tf_op args[14]
  2.6 39.0 %mesh_steps.1 = (bf16[1024,128]{1,0:T(8,128)(2,1)}, bf16[4096,128]{1,0:T(8,128)(2,1)}) custom-call(bf16[1024,128]{1,0:T(8,128)(2,1)} %node_ref.1, bf16[4096,128]{1,0:T(8,128)(2,1)} %edge_ref.1, s32[32,128]{1,0:T(8,128)} %bitcast.4, s32[32,128]{1,0:T(8,128)} %bitcast.5, s32[4,128]{1,0:T(4,128)} %bitcast.7, bf16[8,128]{1,0:T(8,128)(2,1)} %ctx_ref.1, ...), custom_call_target="tpu_custom_call" | custom-call | tf_op jit(solution)/shard_map/mesh_steps/pallas_call | solution.py:313
  41.6 1.7 %copy.22 = bf16[1024,128]{1,0:T(8,128)(2,1)} copy(bf16[1024,128]{1,0:T(8,128)(2,1)} %get-tuple-element.4) | data formatting | bytes 524288
  43.3 2.3 %copy.23 = bf16[4096,128]{1,0:T(8,128)(2,1)} copy(bf16[4096,128]{1,0:T(8,128)(2,1)} %get-tuple-element.5) | data formatting | bytes 2097152
Async XLA Ops:
  0.6 0.7 %copy-start = (f32[2,3,128]{2,0,1:T(2,128)S(1)}, f32[2,3,128]{2,0,1:T(2,128)}, u32[]{:S(2)}) copy-start(f32[2,3,128]{2,0,1:T(2,128)} %param.25) | copy-start | bytes 9220
  1.3 0.7 %copy-start.1 = (f32[2,3,128]{2,0,1:T(2,128)S(1)}, f32[2,3,128]{2,0,1:T(2,128)}, u32[]{:S(2)}) copy-start(f32[2,3,128]{2,0,1:T(2,128)} %param.30) | copy-start | bytes 9220

commit v2 on v1

--- a/solution.py
+++ b/solution.py
@@ -33,14 +33,25 @@
     return jnp.where(mask, 1.0, 0.0).astype(BF16)
 
 
+def pick_parts(index, axis, count):
+    base = hot((index & (LANES - 1)) == iota(axis))
+    group = (index >> 7).astype(F32).astype(BF16)
+    zero = jnp.zeros_like(base)
+    return [
+        jnp.where(group == jnp.asarray(part, BF16), base, zero) for part in range(count // LANES)
+    ]
+
+
 def pick_rows(column, count):
-    lanes = iota(1)
-    parts = [hot(column == lanes + start) for start in range(0, count, LANES)]
-    return jnp.concatenate(parts, axis=1)
-
-
-def norm(y_val, gain, shift):
-    centred = y_val - jnp.mean(y_val, axis=-1, keepdims=True)
+    return jnp.concatenate(pick_parts(column, 1, count), axis=1)
+
+
+def centre(values):
+    values = values.astype(F32)
+    return values - jnp.mean(values, axis=-1, keepdims=True)
+
+
+def norm(centred, gain, shift):
     spread = jnp.mean(centred * centred, axis=-1, keepdims=True)
     return centred * lax.rsqrt(spread + EPS) * gain + shift
 
@@ -66,8 +77,7 @@
     ng,
     node_out,
     edge_out,
-    hot_send,
-    hot_recv,
+    operand,
     hot_sum,
     side_send,
     side_recv,
@@ -75,10 +85,12 @@
     picked,
     halo,
     table,
-    from_ext,
-    from_own,
+    weights,
     sums,
     ctx_part,
+    even_part,
+    odd_part,
+    edge_sem,
     halo_send_sem,
     halo_recv_sem,
     row_send_sem,
@@ -93,6 +105,11 @@
     ext = nodes + 4 * count
     half_ext, half_own = ext // 2, nodes // 2
     ctx_rows = ctx_ref.shape[0]
+    at_recv, at_edge = half_ext, half_ext + nodes
+    edge_in = pltpu.make_async_copy(
+        edge_ref, operand.at[:, at_edge : at_edge + width], edge_sem
+    )
+    edge_in.start()
     per_block = BLOCK // LANES
 
     barrier = pltpu.get_barrier_semaphore()
@@ -181,19 +198,19 @@
             send_row = send_ref[pl.ds(line, 1), :]
             recv_row = recv_ref[pl.ds(line, 1), :]
             rows = pl.ds(pl.multiple_of(line * LANES, LANES), LANES)
-            send = as_column(send_row)
-            recv = as_column(recv_row)
+            both = as_column(send_row + (recv_row << 16))
+            send, recv = both & 0xFFFF, both >> 16
             send_high = (send >= half_ext).astype(jnp.int32)
-            recv_high = (recv >= half_own).astype(jnp.int32)
             side_send[rows, :] = send_high
-            side_recv[rows, :] = recv_high
-            hot_send[rows, :] = pick_rows(send - send_high * half_ext, half_ext)
-            hot_recv[rows, :] = pick_rows(recv - recv_high * half_own, half_own)
+            side_recv[rows, :] = (recv >= half_own).astype(jnp.int32)
+            operand[rows, :at_recv] = pick_rows(send - send_high * half_ext, half_ext)
+            operand[rows, at_recv:at_edge] = pick_rows(recv, nodes)
             recv_low = recv_row - (recv_row >= half_own).astype(jnp.int32) * half_own
-            for start in range(0, half_own, LANES):
-                hot_sum[block, start : start + LANES, sub * LANES : (sub + 1) * LANES] = hot(
-                    iota(0) + start == recv_low
-                )
+            recv_low = jnp.broadcast_to(recv_low, (LANES, LANES))
+            for part, value in enumerate(pick_parts(recv_low, 0, half_own)):
+                hot_sum[
+                    block, part * LANES : (part + 1) * LANES, sub * LANES : (sub + 1) * LANES
+                ] = value
         return carry
 
     lax.fori_loop(0, edges // BLOCK, prepare, 0)
@@ -206,34 +223,49 @@
     def fill_own(layer, now):
         w_pair = jnp.concatenate([ew1[layer, :width], ew1[layer, width : 2 * width]], axis=1)
         both = mm(now[...], w_pair).astype(BF16)
-        from_ext[:, :width] = both[:half_ext, :width]
-        from_ext[: nodes - half_ext, width:] = both[half_ext:, :width]
-        from_own[:, :width] = both[:half_own, width:]
-        from_own[:, width:] = both[half_own:, width:]
-
-    def edge_phase(layer, source):
-        from_ext[nodes - half_ext :, width:] = mm(halo[layer], ew1[layer, :width]).astype(BF16)
+        weights[:half_ext, :width] = both[:half_ext, :width]
+        weights[: nodes - half_ext, width:] = both[half_ext:, :width]
+        for start in (0, width):
+            weights[at_recv:at_edge, start : start + width] = both[:, width:]
+            weights[at_edge:, start : start + width] = ew1[layer, 2 * width :]
+
+    def edge_phase(layer):
+        weights[nodes - half_ext : half_ext, width:] = mm(halo[layer], ew1[layer, :width]).astype(
+            BF16
+        )
         sums[...] = jnp.zeros_like(sums)
-
-        def body(block, carry):
+        odd_part[...] = jnp.zeros_like(odd_part)
+        w_out = centre(ew2[layer]).astype(BF16)
+        b_out = centre(eb[1, layer : layer + 1])
+
+        def gather(block, target):
             rows = pl.ds(pl.multiple_of(block * BLOCK, BLOCK), BLOCK)
-            old = source[rows, :]
-            by_send = mm(hot_send[rows, :], from_ext[...])
-            by_recv = mm(hot_recv[rows, :], from_own[...])
+            pre = mm(operand[rows, :], weights[...])
+            pre = jnp.where(side_send[rows, :] > 0, pre[:, width:], pre[:, :width])
+            hidden = jnp.maximum(pre + eb[0, layer : layer + 1], 0.0).astype(BF16)
+            centred = mm(hidden, w_out) + b_out
+            new = operand[rows, at_edge:].astype(F32)
+            new += norm(centred, eg[layer : layer + 1], eb[2, layer : layer + 1])
+            if layer == LAYERS - 1:
+                edge_out[rows, :] = new.astype(BF16)
+            else:
+                operand[rows, at_edge:] = new.astype(BF16)
             high = side_recv[rows, :] > 0
-            pre = mm(old, ew1[layer, 2 * width :]) + eb[layer, 0:1]
-            pre += jnp.where(side_send[rows, :] > 0, by_send[:, width:], by_send[:, :width])
-            pre += jnp.where(high, by_recv[:, width:], by_recv[:, :width])
-            hidden = jnp.maximum(pre, 0.0).astype(BF16)
-            y_val = mm(hidden, ew2[layer]) + eb[layer, 1:2]
-            new = old.astype(F32) + norm(y_val, eg[layer : layer + 1], eb[layer, 2:3])
-            edge_out[rows, :] = new.astype(BF16)
-            low_part = jnp.where(high, 0.0, new).astype(BF16)
-            high_part = jnp.where(high, new, 0.0).astype(BF16)
-            sums[...] += mm(hot_sum[block], jnp.concatenate([low_part, high_part], axis=1))
+            target[:, :width] = jnp.where(high, 0.0, new).astype(BF16)
+            target[:, width:] = jnp.where(high, new, 0.0).astype(BF16)
+
+        def scatter(block, source):
+            sums[...] += mm(hot_sum[block], source[...])
+
+        def body(pair, carry):
+            scatter(jnp.maximum(2 * pair - 1, 0), odd_part)
+            gather(2 * pair, even_part)
+            scatter(2 * pair, even_part)
+            gather(2 * pair + 1, odd_part)
             return carry
 
-        lax.fori_loop(0, edges // BLOCK, body, 0)
+        lax.fori_loop(0, edges // (2 * BLOCK), body, 0)
+        scatter(edges // BLOCK - 1, odd_part)
 
     def node_phase(layer, now, shift_in):
         summed = jnp.concatenate([sums[:, :width], sums[:, width:]], axis=0).astype(BF16)
@@ -241,13 +273,15 @@
         pre = mm(feats, nw1[layer, : 2 * width]) + shift_in
         pre += ctx_part[:, layer * width : (layer + 1) * width]
         hidden = jnp.maximum(pre, 0.0).astype(BF16)
-        y_val = mm(hidden, nw2[layer]) + nb[layer, 1:2]
-        new = now[...].astype(F32) + norm(y_val, ng[layer : layer + 1], nb[layer, 2:3])
+        centred = mm(hidden, centre(nw2[layer]).astype(BF16)) + centre(nb[1, layer : layer + 1])
+        new = now[...].astype(F32)
+        new += norm(centred, ng[layer : layer + 1], nb[2, layer : layer + 1])
         node_out[...] = new.astype(BF16)
 
     fill_own(0, node_ref)
     halo_wait(0)
-    edge_phase(0, edge_ref)
+    edge_in.wait()
+    edge_phase(0)
 
     for step in range(1, n_col):
         col_copy(step, lax.rem(my_col + n_col - step, n_col)).wait_recv()
@@ -265,7 +299,7 @@
         picker = pick_rows(as_column(region_ref[line : line + 1, :]), regions)
         ctx_part[line * LANES : (line + 1) * LANES, :] = mm(picker, projected)
     shifts = [
-        nb[l, 0:1]
+        nb[0, l : l + 1]
         + jnp.dot(
             pooled, nwg[l].astype(F32), precision=lax.Precision.HIGHEST, preferred_element_type=F32
         )
@@ -277,7 +311,7 @@
     halo_start(1)
     fill_own(1, node_out)
     halo_wait(1)
-    edge_phase(1, edge_out)
+    edge_phase(1)
     node_phase(1, node_out, shifts[1])
 
     for layer in range(LAYERS):
@@ -299,6 +333,7 @@
     edges = edge.shape[0]
     count = index.shape[2]
     half_ext, half_own = (nodes + 4 * count) // 2, nodes // 2
+    deep = half_ext + nodes + width
     vmem = pl.BlockSpec(memory_space=pltpu.VMEM)
     dma = pltpu.SemaphoreType.DMA
     operands = (
@@ -310,17 +345,19 @@
         ctx,
         region.reshape(nodes // LANES, LANES),
     ) + args[7:]
+    operands = tuple(
+        jnp.transpose(x, (1, 0, 2)) if x.shape == (LAYERS, 3, width) else x for x in operands
+    )
     return pl.pallas_call(
         functools.partial(kernel, n_row, n_col),
         out_shape=(
             jax.ShapeDtypeStruct(node.shape, BF16),
             jax.ShapeDtypeStruct(edge.shape, BF16),
         ),
-        in_specs=[vmem] * len(operands),
+        in_specs=[vmem, pl.BlockSpec(memory_space=pl.ANY)] + [vmem] * (len(operands) - 2),
         out_specs=(vmem, vmem),
         scratch_shapes=[
-            pltpu.VMEM((edges, half_ext), BF16),
-            pltpu.VMEM((edges, half_own), BF16),
+            pltpu.VMEM((edges, deep), BF16),
             pltpu.VMEM((edges // BLOCK, half_own, BLOCK), BF16),
             pltpu.VMEM((edges, width), jnp.int32),
             pltpu.VMEM((edges, width), jnp.int32),
@@ -328,10 +365,12 @@
             pltpu.VMEM((LAYERS, 4 * count, width), BF16),
             pltpu.VMEM((LAYERS, 4 * count, width), BF16),
             pltpu.VMEM((n_col, n_row, ctx.shape[0] + 8, width), F32),
-            pltpu.VMEM((half_ext, 2 * width), BF16),
-            pltpu.VMEM((half_own, 2 * width), BF16),
+            pltpu.VMEM((deep, 2 * width), BF16),
             pltpu.VMEM((half_own, 2 * width), F32),
             pltpu.VMEM((nodes, LAYERS * width), F32),
+            pltpu.VMEM((BLOCK, 2 * width), BF16),
+            pltpu.VMEM((BLOCK, 2 * width), BF16),
+            dma(()),
             dma((LAYERS, 4)),
             dma((LAYERS, 4)),
             dma((n_row - 1,)),

time: 45.8 us -> 50.3 us (1.098)
  Pallas kernels: 39 us -> 45.6 us
  local copies, waits for them, and re-layouts: 5.89 us -> 3.93 us
    pallas_call x1, Pallas kernels: 39 us -> 45.6 us  [local(): pl.pallas_call(functools.partial(kernel, n_row, n_col), out_shape=(jax.Sh...]
    unnamed x8 -> x2, local copies, waits for them, and re-layouts: 5.89 us -> 3.93 us
where the time goes in v2:
time: 50.3 us; the launch traced here: 50.1 us
  Pallas kernels  45.6 us (91%)
  local copies, waits for them, and re-layouts  3.93 us (8%)
  between operations  0.65 us (1%)
    pallas_call x1, Pallas kernels, local(): pl.pallas_call(functools.partial(kernel, n_row, n_col), out_shape=(jax.Sh...  45.6 us
    unnamed x2, local copies, waits for them, and re-layouts  3.93 us

profile of v2, /device:TPU:0, one launch (start us, length us, event | category | flops | bytes accessed | tf_op | source)
XLA Modules:
  0.0 50.1 jit_solution(7714243210225763705)
XLA Ops:
  0.6 45.6 %mesh_steps.1 = (bf16[1024,128]{1,0:T(8,128)(2,1)}, bf16[4096,128]{1,0:T(8,128)(2,1)}) custom-call(bf16[1024,128]{1,0:T(8,128)(2,1)} %node_ref.1, bf16[4096,128]{1,0:T(8,128)(2,1)} %edge_ref.1, s32[32,128]{1,0:T(8,128)} %bitcast.6, s32[32,128]{1,0:T(8,128)} %bitcast.7, s32[4,128]{1,0:T(4,128)} %bitcast.11, bf16[8,128]{1,0:T(8,128)(2,1)} %ctx_ref.1, ...), custom_call_target="tpu_custom_call" | custom-call | tf_op jit(solution)/shard_map/mesh_steps/pallas_call | solution.py:351
  46.2 1.7 %copy.20 = bf16[1024,128]{1,0:T(8,128)(2,1)} copy(bf16[1024,128]{1,0:T(8,128)(2,1)} %get-tuple-element.4) | data formatting | bytes 524288
  47.9 2.3 %copy.21 = bf16[4096,128]{1,0:T(8,128)(2,1)} copy(bf16[4096,128]{1,0:T(8,128)(2,1)} %get-tuple-element.5) | data formatting | bytes 2097152

commit v3 on v2

--- a/solution.py
+++ b/solution.py
@@ -49,6 +49,12 @@
 def centre(values):
     values = values.astype(F32)
     return values - jnp.mean(values, axis=-1, keepdims=True)
+
+
+def twice(weight):
+    zero = jnp.zeros_like(weight)
+    top = jnp.concatenate([weight, zero], axis=1)
+    return jnp.concatenate([top, jnp.concatenate([zero, weight], axis=1)], axis=0)
 
 
 def norm(centred, gain, shift):
@@ -77,7 +83,8 @@
     ng,
     node_out,
     edge_out,
-    operand,
+    hot_send,
+    hot_recv,
     hot_sum,
     side_send,
     side_recv,
@@ -85,11 +92,11 @@
     picked,
     halo,
     table,
-    weights,
+    from_ext,
+    from_own,
     sums,
     ctx_part,
-    even_part,
-    odd_part,
+    parts,
     edge_sem,
     halo_send_sem,
     halo_recv_sem,
@@ -105,12 +112,9 @@
     ext = nodes + 4 * count
     half_ext, half_own = ext // 2, nodes // 2
     ctx_rows = ctx_ref.shape[0]
-    at_recv, at_edge = half_ext, half_ext + nodes
-    edge_in = pltpu.make_async_copy(
-        edge_ref, operand.at[:, at_edge : at_edge + width], edge_sem
-    )
+    edge_in = pltpu.make_async_copy(edge_ref, edge_out, edge_sem)
     edge_in.start()
-    per_block = BLOCK // LANES
+    per_block = 2 * BLOCK // LANES
 
     barrier = pltpu.get_barrier_semaphore()
     for step in range(1, n_row):
@@ -202,9 +206,10 @@
             send, recv = both & 0xFFFF, both >> 16
             send_high = (send >= half_ext).astype(jnp.int32)
             side_send[rows, :] = send_high
-            side_recv[rows, :] = (recv >= half_own).astype(jnp.int32)
-            operand[rows, :at_recv] = pick_rows(send - send_high * half_ext, half_ext)
-            operand[rows, at_recv:at_edge] = pick_rows(recv, nodes)
+            recv_high = (recv >= half_own).astype(jnp.int32)
+            side_recv[rows, :] = recv_high
+            hot_send[rows, :] = pick_rows(send - send_high * half_ext, half_ext)
+            hot_recv[rows, :] = pick_rows(recv - recv_high * half_own, half_own)
             recv_low = recv_row - (recv_row >= half_own).astype(jnp.int32) * half_own
             recv_low = jnp.broadcast_to(recv_low, (LANES, LANES))
             for part, value in enumerate(pick_parts(recv_low, 0, half_own)):
@@ -213,7 +218,7 @@
                 ] = value
         return carry
 
-    lax.fori_loop(0, edges // BLOCK, prepare, 0)
+    lax.fori_loop(0, edges // (2 * BLOCK), prepare, 0)
 
     for step in range(1, n_row):
         row_copy(step, lax.rem(my_row + n_row - step, n_row)).wait_recv()
@@ -223,49 +228,57 @@
     def fill_own(layer, now):
         w_pair = jnp.concatenate([ew1[layer, :width], ew1[layer, width : 2 * width]], axis=1)
         both = mm(now[...], w_pair).astype(BF16)
-        weights[:half_ext, :width] = both[:half_ext, :width]
-        weights[: nodes - half_ext, width:] = both[half_ext:, :width]
-        for start in (0, width):
-            weights[at_recv:at_edge, start : start + width] = both[:, width:]
-            weights[at_edge:, start : start + width] = ew1[layer, 2 * width :]
+        from_ext[:, :width] = both[:half_ext, :width]
+        from_ext[: nodes - half_ext, width:] = both[half_ext:, :width]
+        from_own[:, :width] = both[:half_own, width:]
+        from_own[:, width:] = both[half_own:, width:]
 
     def edge_phase(layer):
-        weights[nodes - half_ext : half_ext, width:] = mm(halo[layer], ew1[layer, :width]).astype(
-            BF16
-        )
+        from_ext[nodes - half_ext :, width:] = mm(halo[layer], ew1[layer, :width]).astype(BF16)
         sums[...] = jnp.zeros_like(sums)
-        odd_part[...] = jnp.zeros_like(odd_part)
-        w_out = centre(ew2[layer]).astype(BF16)
+        parts[...] = jnp.zeros_like(parts)
+        w_edge = twice(ew1[layer, 2 * width :])
+        w_out = twice(centre(ew2[layer]).astype(BF16))
+        b_in = eb[0, layer : layer + 1]
         b_out = centre(eb[1, layer : layer + 1])
 
-        def gather(block, target):
-            rows = pl.ds(pl.multiple_of(block * BLOCK, BLOCK), BLOCK)
-            pre = mm(operand[rows, :], weights[...])
-            pre = jnp.where(side_send[rows, :] > 0, pre[:, width:], pre[:, :width])
-            hidden = jnp.maximum(pre + eb[0, layer : layer + 1], 0.0).astype(BF16)
-            centred = mm(hidden, w_out) + b_out
-            new = operand[rows, at_edge:].astype(F32)
-            new += norm(centred, eg[layer : layer + 1], eb[2, layer : layer + 1])
-            if layer == LAYERS - 1:
+        def scatter(pair):
+            sums[...] += mm(hot_sum[pair], parts[...])
+
+        def body(pair, carry):
+            blocks = [
+                pl.ds(pl.multiple_of((2 * pair + half) * BLOCK, BLOCK), BLOCK) for half in range(2)
+            ]
+            old = [edge_out[rows, :] for rows in blocks]
+            by_edge = mm(jnp.concatenate(old, axis=1), w_edge)
+            by_send = [mm(hot_send[rows, :], from_ext[...]) for rows in blocks]
+            by_recv = [mm(hot_recv[rows, :], from_own[...]) for rows in blocks]
+            scatter(jnp.maximum(pair - 1, 0))
+            hidden = []
+            for half, rows in enumerate(blocks):
+                pre = by_edge[:, half * width : (half + 1) * width] + b_in
+                pre += jnp.where(
+                    side_send[rows, :] > 0, by_send[half][:, width:], by_send[half][:, :width]
+                )
+                pre += jnp.where(
+                    side_recv[rows, :] > 0, by_recv[half][:, width:], by_recv[half][:, :width]
+                )
+                hidden.append(jnp.maximum(pre, 0.0).astype(BF16))
+            y_val = mm(jnp.concatenate(hidden, axis=1), w_out)
+            for half, rows in enumerate(blocks):
+                centred = y_val[:, half * width : (half + 1) * width] + b_out
+                new = old[half].astype(F32)
+                new += norm(centred, eg[layer : layer + 1], eb[2, layer : layer + 1])
                 edge_out[rows, :] = new.astype(BF16)
-            else:
-                operand[rows, at_edge:] = new.astype(BF16)
-            high = side_recv[rows, :] > 0
-            target[:, :width] = jnp.where(high, 0.0, new).astype(BF16)
-            target[:, width:] = jnp.where(high, new, 0.0).astype(BF16)
-
-        def scatter(block, source):
-            sums[...] += mm(hot_sum[block], source[...])
-
-        def body(pair, carry):
-            scatter(jnp.maximum(2 * pair - 1, 0), odd_part)
-            gather(2 * pair, even_part)
-            scatter(2 * pair, even_part)
-            gather(2 * pair + 1, odd_part)
+                high = side_recv[rows, :] > 0
+                place = slice(half * BLOCK, (half + 1) * BLOCK)
+                parts[place, :width] = jnp.where(high, 0.0, new).astype(BF16)
+                parts[place, width:] = jnp.where(high, new, 0.0).astype(BF16)
             return carry
 
-        lax.fori_loop(0, edges // (2 * BLOCK), body, 0)
-        scatter(edges // BLOCK - 1, odd_part)
+        pairs = edges // (2 * BLOCK)
+        lax.fori_loop(0, pairs, body, 0)
+        scatter(pairs - 1)
 
     def node_phase(layer, now, shift_in):
         summed = jnp.concatenate([sums[:, :width], sums[:, width:]], axis=0).astype(BF16)
@@ -333,7 +346,6 @@
     edges = edge.shape[0]
     count = index.shape[2]
     half_ext, half_own = (nodes + 4 * count) // 2, nodes // 2
-    deep = half_ext + nodes + width
     vmem = pl.BlockSpec(memory_space=pltpu.VMEM)
     dma = pltpu.SemaphoreType.DMA
     operands = (
@@ -357,19 +369,20 @@
         in_specs=[vmem, pl.BlockSpec(memory_space=pl.ANY)] + [vmem] * (len(operands) - 2),
         out_specs=(vmem, vmem),
         scratch_shapes=[
-            pltpu.VMEM((edges, deep), BF16),
-            pltpu.VMEM((edges // BLOCK, half_own, BLOCK), BF16),
+            pltpu.VMEM((edges, half_ext), BF16),
+            pltpu.VMEM((edges, half_own), BF16),
+            pltpu.VMEM((edges // (2 * BLOCK), half_own, 2 * BLOCK), BF16),
             pltpu.VMEM((edges, width), jnp.int32),
             pltpu.VMEM((edges, width), jnp.int32),
             pltpu.VMEM((4 * count, nodes), BF16),
             pltpu.VMEM((LAYERS, 4 * count, width), BF16),
             pltpu.VMEM((LAYERS, 4 * count, width), BF16),
             pltpu.VMEM((n_col, n_row, ctx.shape[0] + 8, width), F32),
-            pltpu.VMEM((deep, 2 * width), BF16),
+            pltpu.VMEM((half_ext, 2 * width), BF16),
+            pltpu.VMEM((half_own, 2 * width), BF16),
             pltpu.VMEM((half_own, 2 * width), F32),
             pltpu.VMEM((nodes, LAYERS * width), F32),
-            pltpu.VMEM((BLOCK, 2 * width), BF16),
-            pltpu.VMEM((BLOCK, 2 * width), BF16),
+            pltpu.VMEM((2 * BLOCK, 2 * width), BF16),
             dma(()),
             dma((LAYERS, 4)),
             dma((LAYERS, 4)),
@@ -379,7 +392,7 @@
             dma((n_col - 1,)),
         ],
         compiler_params=pltpu.CompilerParams(
-            collective_id=0, has_side_effects=True, vmem_limit_bytes=56 * 1024 * 1024
+            collective_id=0, has_side_effects=True, vmem_limit_bytes=36 * 1024 * 1024
         ),
         name="mesh_steps",
     )(*operands)

time: 50.3 us -> 42.4 us (0.84)
  Pallas kernels: 45.6 us -> 28.7 us
  local copies, waits for them, and re-layouts: 3.93 us -> 12.4 us
    pallas_call x1, Pallas kernels: 45.6 us -> 28.7 us  [local(): pl.pallas_call(functools.partial(kernel, n_row, n_col), out_shape=(jax.Sh...]
    unnamed x2 -> x34, local copies, waits for them, and re-layouts: 3.93 us -> 12.4 us
where the time goes in v3:
time: 42.4 us; the launch traced here: 41.8 us
  Pallas kernels  28.7 us (68%)
  local copies, waits for them, and re-layouts  12.4 us (29%)
  between operations  0.69 us (2%)
    pallas_call x1, Pallas kernels, local(): pl.pallas_call(functools.partial(kernel, n_row, n_col), out_shape=(jax.Sh...  28.7 us
    unnamed x34, local copies, waits for them, and re-layouts  12.4 us

profile of v3, /device:TPU:0, one launch (start us, length us, event | category | flops | bytes accessed | tf_op | source)
XLA Modules:
  0.0 41.8 jit_solution(17645367243446379931)
XLA Ops:
  0.6 0.0 copy-start.11
  0.6 0.0 copy-start.14
  0.7 0.0 copy-start.9
  0.7 0.0 copy-start.10
  0.7 0.6 %copy-done.11 = f32[2,3,128]{2,0,1:T(2,128)S(1)} copy-done((f32[2,3,128]{2,0,1:T(2,128)S(1)}, f32[2,3,128]{2,0,1:T(2,128)}, u32[]{:S(2)}) %copy-start.11) | copy-done | bytes 3096
  1.3 0.0 copy-done.14
  1.3 0.0 copy-done.9
  1.4 0.0 copy-done.10
  1.4 0.0 copy-start
  1.4 1.2 %copy-done = bf16[4096,128]{1,0:T(8,128)(2,1)S(1)} copy-done((bf16[4096,128]{1,0:T(8,128)(2,1)S(1)}, bf16[4096,128]{1,0:T(8,128)(2,1)}, u32[]{:S(2)}) %copy-start) | copy-done | bytes 1048600
  2.6 0.9 %copy-done.1 = bf16[1024,128]{1,0:T(8,128)(2,1)S(1)} copy-done((bf16[1024,128]{1,0:T(8,128)(2,1)S(1)}, bf16[1024,128]{1,0:T(8,128)(2,1)}, u32[]{:S(2)}) %copy-start.1) | copy-done | bytes 262168
  3.5 0.0 copy-start.2
  3.5 0.9 %copy-done.2 = bf16[2,384,128]{2,1,0:T(8,128)(2,1)S(1)} copy-done((bf16[2,384,128]{2,1,0:T(8,128)(2,1)S(1)}, bf16[2,384,128]{2,1,0:T(8,128)(2,1)}, u32[]{:S(2)}) %copy-start.2) | copy-done | bytes 196632
  4.5 0.0 copy-start.3
  4.5 0.9 %copy-done.3 = bf16[2,384,128]{2,1,0:T(8,128)(2,1)S(1)} copy-done((bf16[2,384,128]{2,1,0:T(8,128)(2,1)S(1)}, bf16[2,384,128]{2,1,0:T(8,128)(2,1)}, u32[]{:S(2)}) %copy-start.3) | copy-done | bytes 196632
  5.4 0.0 copy-start.4
  5.4 0.8 %copy-done.4 = bf16[2,128,128]{2,1,0:T(8,128)(2,1)S(1)} copy-done((bf16[2,128,128]{2,1,0:T(8,128)(2,1)S(1)}, bf16[2,128,128]{2,1,0:T(8,128)(2,1)}, u32[]{:S(2)}) %copy-start.4) | copy-done | bytes 65560
  6.2 0.0 copy-start.5
  6.2 0.8 %copy-done.5 = bf16[2,128,128]{2,1,0:T(8,128)(2,1)S(1)} copy-done((bf16[2,128,128]{2,1,0:T(8,128)(2,1)S(1)}, bf16[2,128,128]{2,1,0:T(8,128)(2,1)}, u32[]{:S(2)}) %copy-start.5) | copy-done | bytes 65560
  7.1 0.0 copy-start.6
  7.1 0.8 %copy-done.6 = bf16[2,128,128]{2,1,0:T(8,128)(2,1)S(1)} copy-done((bf16[2,128,128]{2,1,0:T(8,128)(2,1)S(1)}, bf16[2,128,128]{2,1,0:T(8,128)(2,1)}, u32[]{:S(2)}) %copy-start.6) | copy-done | bytes 65560
  7.9 0.0 copy-start.7
  7.9 0.7 %copy-done.7 = s32[4096]{0:T(1024)S(1)} copy-done((s32[4096]{0:T(1024)S(1)}, s32[4096]{0:T(1024)}, u32[]{:S(2)}) %copy-start.7) | copy-done | bytes 16408
  8.6 0.0 copy-start.8
  8.6 0.7 %copy-done.8 = s32[4096]{0:T(1024)S(1)} copy-done((s32[4096]{0:T(1024)S(1)}, s32[4096]{0:T(1024)}, u32[]{:S(2)}) %copy-start.8) | copy-done | bytes 16408
  9.4 0.0 copy-start.12
  9.4 0.7 %copy-done.12 = s32[1,4,128]{2,1,0:T(4,128)S(1)} copy-done((s32[1,4,128]{2,1,0:T(4,128)S(1)}, s32[1,4,128]{2,1,0:T(4,128)}, u32[]{:S(2)}) %copy-start.12) | copy-done | bytes 2072
  10.0 0.7 %copy-done.13 = bf16[8,128]{1,0:T(8,128)(2,1)S(1)} copy-done((bf16[8,128]{1,0:T(8,128)(2,1)S(1)}, bf16[8,128]{1,0:T(8,128)(2,1)}, u32[]{:S(2)}) %copy-start.13) | copy-done | bytes 2072
  10.7 0.7 %copy-done.15 = f32[2,128]{1,0:T(2,128)S(1)} copy-done((f32[2,128]{1,0:T(2,128)S(1)}, f32[2,128]{1,0:T(2,128)}, u32[]{:S(2)}) %copy-start.15) | copy-done | bytes 1048
  11.4 28.7 %mesh_steps.1 = (bf16[1024,128]{1,0:T(8,128)(2,1)S(1)}, bf16[4096,128]{1,0:T(8,128)(2,1)S(1)}) custom-call(bf16[1024,128]{1,0:T(8,128)(2,1)S(1)} %copy-done.1, bf16[4096,128]{1,0:T(8,128)(2,1)S(1)} %copy-done, s32[32,128]{1,0:T(8,128)S(1)} %bitcast.6, s32[32,128]{1,0:T(8,128)S(1)} %bitcast.7, s32[4,128]{1,0:T(4,128)S(1)} %bitcast.11, ...), custom_call_target="tpu_custom_call" | custom-call | tf_op jit(solution)/shard_map/mesh_steps/pallas_call | solution.py:363
  40.1 0.7 %copy.20 = bf16[1024,128]{1,0:T(8,128)(2,1)} copy(bf16[1024,128]{1,0:T(8,128)(2,1)S(1)} %get-tuple-element.4) | data formatting | bytes 524288
  40.8 1.0 %copy.21 = bf16[4096,128]{1,0:T(8,128)(2,1)} copy(bf16[4096,128]{1,0:T(8,128)(2,1)S(1)} %get-tuple-element.5) | data formatting | bytes 2097152
  (3 shorter events, 0.0 us)
Async XLA Ops:
  0.6 0.7 %copy-start.11 = (f32[2,3,128]{2,0,1:T(2,128)S(1)}, f32[2,3,128]{2,0,1:T(2,128)}, u32[]{:S(2)}) copy-start(f32[2,3,128]{2,0,1:T(2,128)} %param.30) | copy-start | bytes 9220
  0.6 0.7 %copy-start.14 = (f32[2,128]{1,0:T(2,128)S(1)}, f32[2,128]{1,0:T(2,128)}, u32[]{:S(2)}) copy-start(f32[2,128]{1,0:T(2,128)} %eg.1) | copy-start | bytes 3076
  0.7 0.7 %copy-start.9 = (s32[1024]{0:T(1024)S(1)}, s32[1024]{0:T(1024)}, u32[]{:S(2)}) copy-start(s32[1024]{0:T(1024)} %param.22) | copy-start | bytes 12292
  0.7 0.7 %copy-start.10 = (f32[2,3,128]{2,0,1:T(2,128)S(1)}, f32[2,3,128]{2,0,1:T(2,128)}, u32[]{:S(2)}) copy-start(f32[2,3,128]{2,0,1:T(2,128)} %param.25) | copy-start | bytes 9220
  1.4 1.2 %copy-start = (bf16[4096,128]{1,0:T(8,128)(2,1)S(1)}, bf16[4096,128]{1,0:T(8,128)(2,1)}, u32[]{:S(2)}) copy-start(bf16[4096,128]{1,0:T(8,128)(2,1)} %edge_ref.1) | copy-start | bytes 3145732
  2.6 0.9 %copy-start.1 = (bf16[1024,128]{1,0:T(8,128)(2,1)S(1)}, bf16[1024,128]{1,0:T(8,128)(2,1)}, u32[]{:S(2)}) copy-start(bf16[1024,128]{1,0:T(8,128)(2,1)} %node_ref.1) | copy-start | bytes 786436
  3.5 0.9 %copy-start.2 = (bf16[2,384,128]{2,1,0:T(8,128)(2,1)S(1)}, bf16[2,384,128]{2,1,0:T(8,128)(2,1)}, u32[]{:S(2)}) copy-start(bf16[2,384,128]{2,1,0:T(8,128)(2,1)} %ew1.1) | copy-start | bytes 589828
  4.5 0.9 %copy-start.3 = (bf16[2,384,128]{2,1,0:T(8,128)(2,1)S(1)}, bf16[2,384,128]{2,1,0:T(8,128)(2,1)}, u32[]{:S(2)}) copy-start(bf16[2,384,128]{2,1,0:T(8,128)(2,1)} %nw1.1) | copy-start | bytes 589828
  5.4 0.8 %copy-start.4 = (bf16[2,128,128]{2,1,0:T(8,128)(2,1)S(1)}, bf16[2,128,128]{2,1,0:T(8,128)(2,1)}, u32[]{:S(2)}) copy-start(bf16[2,128,128]{2,1,0:T(8,128)(2,1)} %ew2.1) | copy-start | bytes 196612
  6.2 0.8 %copy-start.5 = (bf16[2,128,128]{2,1,0:T(8,128)(2,1)S(1)}, bf16[2,128,128]{2,1,0:T(8,128)(2,1)}, u32[]{:S(2)}) copy-start(bf16[2,128,128]{2,1,0:T(8,128)(2,1)} %nwg.1) | copy-start | bytes 196612
  7.1 0.8 %copy-start.6 = (bf16[2,128,128]{2,1,0:T(8,128)(2,1)S(1)}, bf16[2,128,128]{2,1,0:T(8,128)(2,1)}, u32[]{:S(2)}) copy-start(bf16[2,128,128]{2,1,0:T(8,128)(2,1)} %nw2.1) | copy-start | bytes 196612
  7.9 0.7 %copy-start.7 = (s32[4096]{0:T(1024)S(1)}, s32[4096]{0:T(1024)}, u32[]{:S(2)}) copy-start(s32[4096]{0:T(1024)} %param.18) | copy-start | bytes 49156
  8.6 0.7 %copy-start.8 = (s32[4096]{0:T(1024)S(1)}, s32[4096]{0:T(1024)}, u32[]{:S(2)}) copy-start(s32[4096]{0:T(1024)} %param.19) | copy-start | bytes 49156
  9.4 0.7 %copy-start.12 = (s32[1,4,128]{2,1,0:T(4,128)S(1)}, s32[1,4,128]{2,1,0:T(4,128)}, u32[]{:S(2)}) copy-start(s32[1,4,128]{2,1,0:T(4,128)} %param.20) | copy-start | bytes 6148
  10.0 0.7 %copy-start.13 = (bf16[8,128]{1,0:T(8,128)(2,1)S(1)}, bf16[8,128]{1,0:T(8,128)(2,1)}, u32[]{:S(2)}) copy-start(bf16[8,128]{1,0:T(8,128)(2,1)} %ctx_ref.1) | copy-start | bytes 6148
  10.7 0.7 %copy-start.15 = (f32[2,128]{1,0:T(2,128)S(1)}, f32[2,128]{1,0:T(2,128)}, u32[]{:S(2)}) copy-start(f32[2,128]{1,0:T(2,128)} %ng.1) | copy-start | bytes 3076

commit v4 on v3

--- a/solution.py
+++ b/solution.py
@@ -65,6 +65,7 @@
 def kernel(
     n_row,
     n_col,
+    rest,
     node_ref,
     edge_ref,
     send_ref,
@@ -195,6 +196,8 @@
     halo_start(0)
     for step in range(1, n_row):
         row_copy(step, my_row).start()
+    for copy in rest:
+        copy.wait()
 
     def prepare(block, carry):
         for sub in range(per_block):
@@ -340,6 +343,29 @@
         col_copy(step, my_col).wait_send()
 
 
+EARLY = (0, 4, 5)
+
+
+def entry(n_row, n_col, count, *refs):
+    given, others = refs[:count], list(refs[count : -count])
+    held, copy_sem = refs[-count:-1], refs[-1]
+    places = list(held)
+    places.insert(1, None)
+    copies = {
+        k: pltpu.make_async_copy(given[k], places[k], copy_sem.at[k])
+        for k in range(count)
+        if k != 1
+    }
+    order = EARLY + tuple(k for k in copies if k not in EARLY)
+    for k in order:
+        copies[k].start()
+    for k in EARLY:
+        copies[k].wait()
+    places[1] = given[1]
+    rest = [copies[k] for k in order if k not in EARLY]
+    kernel(n_row, n_col, rest, *places, *others)
+
+
 def local(n_row, n_col, *args):
     node, edge, send, recv, index, ctx, region = args[:7]
     nodes, width = node.shape
@@ -360,13 +386,14 @@
     operands = tuple(
         jnp.transpose(x, (1, 0, 2)) if x.shape == (LAYERS, 3, width) else x for x in operands
     )
+    operands = tuple(pltpu.with_memory_space_constraint(x, pltpu.HBM) for x in operands)
     return pl.pallas_call(
-        functools.partial(kernel, n_row, n_col),
+        functools.partial(entry, n_row, n_col, len(operands)),
         out_shape=(
             jax.ShapeDtypeStruct(node.shape, BF16),
             jax.ShapeDtypeStruct(edge.shape, BF16),
         ),
-        in_specs=[vmem, pl.BlockSpec(memory_space=pl.ANY)] + [vmem] * (len(operands) - 2),
+        in_specs=[pl.BlockSpec(memory_space=pltpu.HBM)] * len(operands),
         out_specs=(vmem, vmem),
         scratch_shapes=[
             pltpu.VMEM((edges, half_ext), BF16),
@@ -390,7 +417,9 @@
             dma((n_row - 1,)),
             dma((n_col - 1,)),
             dma((n_col - 1,)),
-        ],
+        ]
+        + [pltpu.VMEM(x.shape, x.dtype) for k, x in enumerate(operands) if k != 1]
+        + [dma((len(operands),))],
         compiler_params=pltpu.CompilerParams(
             collective_id=0, has_side_effects=True, vmem_limit_bytes=36 * 1024 * 1024
         ),

time: 42.4 us -> 32.1 us (0.76); the launches traced: 41.8 us -> 31.9 us
  local copies, waits for them, and re-layouts: 12.4 us -> 1.67 us
  Pallas kernels: 28.7 us -> 29.6 us
    unnamed x34 -> x2, local copies, waits for them, and re-layouts: 12.4 us -> 1.67 us
    pallas_call x1, Pallas kernels: 28.7 us -> 29.6 us  [local(): pl.pallas_call(functools.partial(entry, n_row, n_col, len(operands)), out...]
where the time goes in v4:
time: 32.1 us; the launch traced here: 31.9 us
  Pallas kernels  29.6 us (92%)
  local copies, waits for them, and re-layouts  1.67 us (5%)
  between operations  0.65 us (2%)
    pallas_call x1, Pallas kernels, local(): pl.pallas_call(functools.partial(entry, n_row, n_col, len(operands)), out...  29.6 us
    unnamed x2, local copies, waits for them, and re-layouts  1.67 us

profile of v4, /device:TPU:0, one launch (start us, length us, event | category | flops | bytes accessed | tf_op | source)
XLA Modules:
  0.0 31.9 jit_solution(12287053872928488713)
XLA Ops:
  0.6 29.6 %mesh_steps.1 = (bf16[1024,128]{1,0:T(8,128)(2,1)S(1)}, bf16[4096,128]{1,0:T(8,128)(2,1)S(1)}) custom-call(bf16[1024,128]{1,0:T(8,128)(2,1)} %refs_0_.1, bf16[4096,128]{1,0:T(8,128)(2,1)} %refs_1_.1, s32[32,128]{1,0:T(8,128)} %bitcast.6, s32[32,128]{1,0:T(8,128)} %bitcast.7, s32[4,128]{1,0:T(4,128)} %bitcast.11, bf16[8,128]{1,0:T(8,128)(2,1)} %refs_5_.1, ...), custom_call_target="tpu_custom_call" | custom-call | tf_op jit(solution)/shard_map/mesh_steps/pallas_call | solution.py:390
  30.3 0.7 %copy.20 = bf16[1024,128]{1,0:T(8,128)(2,1)} copy(bf16[1024,128]{1,0:T(8,128)(2,1)S(1)} %get-tuple-element.4) | data formatting | bytes 524288
  31.0 1.0 %copy.21 = bf16[4096,128]{1,0:T(8,128)(2,1)} copy(bf16[4096,128]{1,0:T(8,128)(2,1)S(1)} %get-tuple-element.5) | data formatting | bytes 2097152

commit v5 on v4

--- a/solution.py
+++ b/solution.py
@@ -314,21 +314,22 @@
     for line in range(nodes // LANES):
         picker = pick_rows(as_column(region_ref[line : line + 1, :]), regions)
         ctx_part[line * LANES : (line + 1) * LANES, :] = mm(picker, projected)
-    shifts = [
-        nb[0, l : l + 1]
-        + jnp.dot(
-            pooled, nwg[l].astype(F32), precision=lax.Precision.HIGHEST, preferred_element_type=F32
-        )
-        for l in range(LAYERS)
-    ]
-    node_phase(0, node_ref, shifts[0])
+    def shift_of(layer):
+        weight = nwg[layer].astype(F32)
+        term = jnp.dot(
+            pooled, weight, precision=lax.Precision.HIGHEST, preferred_element_type=F32
+        )
+        return nb[0, layer : layer + 1] + term
+
+    node_phase(0, node_ref, shift_of(0))
 
     picked[1] = mm(hot_index[...], node_out[...]).astype(BF16)
     halo_start(1)
     fill_own(1, node_out)
+    last_shift = shift_of(1)
     halo_wait(1)
     edge_phase(1)
-    node_phase(1, node_out, shifts[1])
+    node_phase(1, node_out, last_shift)
 
     for layer in range(LAYERS):
         for side in range(4):

time: 32.1 us -> 32 us (level)
  no operation moved by 1% of the time
where the time goes in v5:
time: 32 us; the launch traced here: 31.9 us
  Pallas kernels  29.5 us (92%)
  local copies, waits for them, and re-layouts  1.67 us (5%)
  between operations  0.65 us (2%)
    pallas_call x1, Pallas kernels, local(): pl.pallas_call(functools.partial(entry, n_row, n_col, len(operands)), out...  29.5 us
    unnamed x2, local copies, waits for them, and re-layouts  1.67 us

profile of v5, /device:TPU:0, one launch (start us, length us, event | category | flops | bytes accessed | tf_op | source)
XLA Modules:
  0.0 31.9 jit_solution(12133607930697316150)
XLA Ops:
  0.6 29.5 %mesh_steps.1 = (bf16[1024,128]{1,0:T(8,128)(2,1)S(1)}, bf16[4096,128]{1,0:T(8,128)(2,1)S(1)}) custom-call(bf16[1024,128]{1,0:T(8,128)(2,1)} %refs_0_.1, bf16[4096,128]{1,0:T(8,128)(2,1)} %refs_1_.1, s32[32,128]{1,0:T(8,128)} %bitcast.6, s32[32,128]{1,0:T(8,128)} %bitcast.7, s32[4,128]{1,0:T(4,128)} %bitcast.11, bf16[8,128]{1,0:T(8,128)(2,1)} %refs_5_.1, ...), custom_call_target="tpu_custom_call" | custom-call | tf_op jit(solution)/shard_map/mesh_steps/pallas_call | solution.py:391
  30.2 0.7 %copy.20 = bf16[1024,128]{1,0:T(8,128)(2,1)} copy(bf16[1024,128]{1,0:T(8,128)(2,1)S(1)} %get-tuple-element.4) | data formatting | bytes 524288
  30.9 1.0 %copy.21 = bf16[4096,128]{1,0:T(8,128)(2,1)} copy(bf16[4096,128]{1,0:T(8,128)(2,1)S(1)} %get-tuple-element.5) | data formatting | bytes 2097152
